TPU v7x, 32 devices: a whole 2x2x4 slice. The times are simulated.
32 devices in a mesh: blk: 8 (over z, x), shard: 4 (over y, core).
Axes of the slice: x: 2, y: 2, z: 4, core: 2. Of those that a mesh axis runs over, the one named last changes fastest.
Arguments:
- tokens: bfloat16 [8192, 2048], P(('blk', 'shard')), may hold values from -6 to 6
- targets: bfloat16 [8192, 2048], P(('blk', 'shard')), may hold values from -6 to 6
- up_weight: bfloat16 [2048, 7168], P(None, 'shard'), may hold values from -0.125 to 0.125
- down_weight: bfloat16 [8, 7168, 2048], P('blk', 'shard'), may hold values from -6 to 6
- mix_numer: int32 [2, 8, 3], replicated, may hold values from 1 to 2, as said below
Outputs:
- drift: bfloat16 [8, 7168, 2048], P('blk', 'shard')
Inputs may be any that keep to these rules, and one draw needn't show every extreme that they name: Each row of mix_numer is (2, 1, 1), (1, 2, 1) or (1, 1, 2).
All inputs are finite; a program needn't handle non-finite values.
Results may differ from a plain program's by a relative error of at most 0.017.
Values may be sent and summed in bfloat16 or wider, within the bound.
No kernel may reach another device: no remote copies, remote signals or barrier semaphores. Data moves between devices by JAX's collectives and lax.ppermute only.
A program may use at most 128 MiB of HBM per device.

v0:
```python
import jax
import jax.numpy as jnp
from jax import lax
from jax.sharding import PartitionSpec as P

FF = 7168
learn_rate = 2.0


def passed_along(x, axis, by):
    devices = lax.axis_size(axis)
    return lax.ppermute(x, axis, [(i, (i + by) % devices) for i in range(devices)])


def combine(center, left, right, weights):
    total = (
        weights[0] * center.astype(jnp.float32)
        + weights[1] * left.astype(jnp.float32)
        + weights[2] * right.astype(jnp.float32)
    )
    return (total / 4.0).astype(jnp.bfloat16)


def numer_of(mix_numer, round_index, worker):
    return lax.dynamic_index_in_dim(mix_numer[round_index], worker, 0, keepdims=False).astype(
        jnp.float32
    )


def body(tokens, targets, up_weight, down_weight, mix_numer):
    weight = down_weight[0]
    out_scale = 1.0 / jnp.sqrt(jnp.float32(FF))
    hidden = jax.nn.silu(
        jnp.dot(
            lax.all_gather(tokens, "shard", axis=0, tiled=True),
            up_weight,
            preferred_element_type=jnp.float32,
        )
    ).astype(jnp.bfloat16)
    rows = hidden
    output = lax.psum_scatter(
        (jnp.dot(rows, weight, preferred_element_type=jnp.float32) * out_scale).astype(
            jnp.bfloat16
        ),
        "shard",
        scatter_dimension=0,
        tiled=True,
    ).astype(jnp.float32)
    resid = (output - targets.astype(jnp.float32)).astype(jnp.bfloat16)
    rows = hidden
    grad = lax.dot_general(
        rows,
        lax.all_gather(resid, "shard", axis=0, tiled=True),
        (((0,), (0,)), ((), ())),
        preferred_element_type=jnp.float32,
    )
    stepped = (weight.astype(jnp.float32) - learn_rate * grad * out_scale).astype(jnp.bfloat16)
    worker = lax.axis_index("blk")
    workers = lax.axis_size("blk")
    near_left = passed_along(stepped, "blk", 1)
    near_right = passed_along(stepped, "blk", -1)
    far_left = passed_along(stepped, "blk", 2)
    far_right = passed_along(stepped, "blk", -2)
    left_worker = (worker - 1) % workers
    right_worker = (worker + 1) % workers
    first_left = combine(near_left, far_left, stepped, numer_of(mix_numer, 0, left_worker))
    first_self = combine(stepped, near_left, near_right, numer_of(mix_numer, 0, worker))
    first_right = combine(near_right, stepped, far_right, numer_of(mix_numer, 0, right_worker))
    mixed = combine(first_self, first_left, first_right, numer_of(mix_numer, 1, worker))
    total = lax.psum(mixed.astype(jnp.float32).astype(jnp.bfloat16), "blk").astype(jnp.float32)
    average = total / jnp.float32(workers)
    return (mixed.astype(jnp.float32) - average).astype(jnp.bfloat16)[None]


def solution(mesh):
    in_specs = (
        P(("blk", "shard"), None),
        P(("blk", "shard"), None),
        P(None, "shard"),
        P("blk", "shard", None),
        P(),
    )
    out_specs = P("blk", "shard", None)
    return jax.shard_map(body, mesh=mesh, in_specs=in_specs, out_specs=out_specs, check_vma=False)
```

profile of v0, /device:TPU:0, one launch (start us, length us, event | category | flops | bytes accessed | tf_op | source)
XLA Modules:
  0.0 932.1 jit_solution(15724398511861249869)
XLA Ops:
  6.5 0.0 all-gather.3.cloned.1.call-start
  6.5 0.7 all-gather.3.cloned.1.call-update
  7.3 0.0 reduce-scatter.2.cloned.1.call-start
  7.3 38.8 %all-gather.3.cloned.1.call-done = bf16[1024,2048]{1,0:T(8,128)(2,1)} async-done(((bf16[256,2048]{1,0:T(8,128)(2,1)}), bf16[1024,2048]{1,0:T(8,128)(2,1)}) %all-gather.3.cloned.1.call-update) | async-done | bytes 4194320 | tf_op jit(solution)/shard_map/all_gather | solution.py:35
  46.1 11.7 %fusion.22 = f32[1024,1792]{1,0:T(8,128)S(1)} fusion(bf16[1024,2048]{1,0:T(8,128)(2,1)} %all-gather.3.cloned.1.call-done, bf16[2048,1792]{1,0:T(8,128)(2,1)} %param.7), kind=kOutput, calls=%fused_computation.37 | convolution fusion | flops 7516192768 | bytes 18874368 | tf_op jit(solution)/shard_map/dot_general | solution.py:34
  57.8 0.0 copy-start.2
  57.8 3.0 copy-done.2
  60.8 0.0 copy-start
  60.8 11.6 %multiply_convert_fusion.1 = bf16[1024,2048]{1,0:T(8,128)(2,1)} fusion(bf16[1,1792,2048]{2,1,0:T(8,128)(2,1)} %param.8, f32[1024,1792]{1,0:T(8,128)S(1)} %fusion.22), kind=kOutput, calls=%fused_computation.22 | convolution fusion | flops 7529562112 | bytes 18874368 | tf_op jit(solution)/shard_map/dot_general | solution.py:42
  72.4 0.0 reduce-scatter.2.cloned.1.call-update
  72.5 0.0 all-gather.5.cloned.1.call-start
  72.5 44.7 %reduce-scatter.2.cloned.1.call-done = bf16[256,2048]{1,0:T(8,128)(2,1)} async-done(((bf16[1024,2048]{1,0:T(8,128)(2,1)}), bf16[256,2048]{1,0:T(8,128)(2,1)}) %reduce-scatter.2.cloned.1.call-update) | async-done | bytes 1048592 | tf_op jit(solution)/shard_map/reduce_scatter | solution.py:41
  117.2 0.0 copy-done
  117.2 2.6 subtract_convert_fusion.2
  119.8 0.0 all-gather.5.cloned.1.call-update
  119.8 0.0 copy-start.1
  119.8 0.0 all-reduce.2.cloned.1.call-start
  119.9 34.5 %all-gather.5.cloned.1.call-done = bf16[1024,2048]{1,0:T(8,128)(2,1)} async-done(((bf16[256,2048]{1,0:T(8,128)(2,1)}), bf16[1024,2048]{1,0:T(8,128)(2,1)}) %all-gather.5.cloned.1.call-update) | async-done | bytes 4194320 | tf_op jit(solution)/shard_map/all_gather | solution.py:53
  154.4 14.9 %subtract_convert_fusion.1 = bf16[1792,2048]{1,0:T(8,128)(2,1)} fusion(bf16[1024,2048]{1,0:T(8,128)(2,1)} %all-gather.5.cloned.1.call-done, bf16[1,1792,2048]{2,1,0:T(8,128)(2,1)} %param.8, f32[1024,1792]{1,0:T(8,128)} %copy-done.2), kind=kOutput, calls=%fused_computation.21 | convolution fusion | flops 7540047872 | bytes 26214400 | tf_op jit(solution)/shard_map/dot_general | solution.py:51
  169.3 3.3 collective-permute-start.3
  172.7 1.4 collective-permute-start.1
  174.1 1.5 collective-permute-start.2
  175.6 0.0 collective-permute-start
  175.6 0.0 copy-done.1
  175.6 0.1 dynamic-slice_convert_fusion.2
  175.7 0.6 fusion.21
  176.3 0.6 fusion.18
  176.9 0.6 fusion.20
  177.5 0.6 fusion.19
  178.1 153.4 %collective-permute-done.3 = bf16[1792,2048]{1,0:T(8,128)(2,1)} collective-permute-done((bf16[1792,2048]{1,0:T(8,128)(2,1)}, bf16[1792,2048]{1,0:T(8,128)(2,1)}, u32[]{:S(2)}, u32[]{:S(2)}) %collective-permute-start.3) | collective-permute-done | bytes 7340064 | tf_op jit(solution)/shard_map/ppermute | solution.py:12
  331.4 157.3 %collective-permute-done.1 = bf16[1792,2048]{1,0:T(8,128)(2,1)} collective-permute-done((bf16[1792,2048]{1,0:T(8,128)(2,1)}, bf16[1792,2048]{1,0:T(8,128)(2,1)}, u32[]{:S(2)}, u32[]{:S(2)}) %collective-permute-start.1) | collective-permute-done | bytes 7340064 | tf_op jit(solution)/shard_map/ppermute | solution.py:12
  488.7 157.5 %collective-permute-done.2 = bf16[1792,2048]{1,0:T(8,128)(2,1)} collective-permute-done((bf16[1792,2048]{1,0:T(8,128)(2,1)}, bf16[1792,2048]{1,0:T(8,128)(2,1)}, u32[]{:S(2)}, u32[]{:S(2)}) %collective-permute-start.2) | collective-permute-done | bytes 7340064 | tf_op jit(solution)/shard_map/ppermute | solution.py:12
  646.3 0.9 collective-permute-done
  647.1 27.4 %multiply_convert_fusion = bf16[1792,2048]{1,0:T(8,128)(2,1)} fusion(bf16[1792,2048]{1,0:T(8,128)(2,1)} %collective-permute-done.3, bf16[1792,2048]{1,0:T(8,128)(2,1)} %subtract_convert_fusion.1, bf16[1792,2048]{1,0:T(8,128)(2,1)} %collective-permute-done.1, bf16[1792,2048]{1,0:T(8,128)(2,1)} %collective-permute-done.2, ...), kind=kLoop, calls=%fused_computation.20 | loop fusion | flops 132120576 | bytes 44040240 | tf_op jit(solution)/shard_map/convert_element_type | solution.py:21
  674.5 0.0 all-reduce.2.cloned.1.call-update
  674.5 238.3 %all-reduce.2.cloned.1.call-done = bf16[1792,2048]{1,0:T(8,128)(2,1)} async-done(((bf16[1792,2048]{1,0:T(8,128)(2,1)}), bf16[1792,2048]{1,0:T(8,128)(2,1)}) %all-reduce.2.cloned.1.call-update) | async-done | bytes 7340048 | tf_op jit(solution)/shard_map/psum | solution.py:70
  912.8 12.7 %fusion.12 = bf16[1,1792,2048]{2,1,0:T(8,128)(2,1)} fusion(bf16[1792,2048]{1,0:T(8,128)(2,1)} %all-reduce.2.cloned.1.call-done, bf16[1792,2048]{1,0:T(8,128)(2,1)} %multiply_convert_fusion), kind=kLoop, calls=%fused_computation.23 | loop fusion | flops 18350080 | bytes 22020096 | tf_op jit(solution)/shard_map/broadcast_in_dim | solution.py:72
  (1 shorter events, 0.0 us)
Async XLA Ops:
  6.5 39.6 %all-gather.3.cloned.1.call-start = ((), (), s32[]{:S(2)}) async-start(), calls=%async_computation.1 | async-start | bytes 5242880 | tf_op jit(solution)/shard_map/all_gather | solution.py:35
  7.3 109.9 %reduce-scatter.2.cloned.1.call-start = ((), (), s32[]{:S(2)}) async-start(), calls=%async_computation.2 | async-start | bytes 5242880 | tf_op jit(solution)/shard_map/reduce_scatter | solution.py:41
  57.8 3.1 copy-start.2
  60.8 56.4 %copy-start = (bf16[256,2048]{1,0:T(8,128)(2,1)S(1)}, bf16[256,2048]{1,0:T(8,128)(2,1)}, u32[]{:S(2)}) copy-start(bf16[256,2048]{1,0:T(8,128)(2,1)} %param.6) | copy-start | bytes 3145732
  72.5 82.0 %all-gather.5.cloned.1.call-start = ((), (), s32[]{:S(2)}) async-start(), calls=%async_computation.3 | async-start | bytes 5242880 | tf_op jit(solution)/shard_map/all_gather | solution.py:53
  119.8 55.8 %copy-start.1 = (s32[2,8,3]{1,0,2:T(2,128)S(1)}, s32[2,8,3]{1,0,2:T(2,128)}, u32[]{:S(2)}) copy-start(s32[2,8,3]{1,0,2:T(2,128)} %param.9) | copy-start | bytes 580
  119.8 793.0 %all-reduce.2.cloned.1.call-start = ((), (), s32[]{:S(2)}) async-start(), calls=%async_computation.4 | async-start | bytes 14680064 | tf_op jit(solution)/shard_map/psum | solution.py:70
  169.3 162.1 %collective-permute-start.3 = (bf16[1792,2048]{1,0:T(8,128)(2,1)}, bf16[1792,2048]{1,0:T(8,128)(2,1)}, u32[]{:S(2)}, u32[]{:S(2)}) collective-permute-start(bf16[1792,2048]{1,0:T(8,128)(2,1)} %subtract_convert_fusion.1), channel_id=1, source_target_pairs={{0,24},{4,28},{8,0},{12,4},{16,8},{20,12},{24,16},{28,20},{1,25},{... | collective-permute-start | bytes 22020104 | tf_op jit(solution)/shard_map/ppermute | solution.py:12
  172.7 316.1 %collective-permute-start.1 = (bf16[1792,2048]{1,0:T(8,128)(2,1)}, bf16[1792,2048]{1,0:T(8,128)(2,1)}, u32[]{:S(2)}, u32[]{:S(2)}) collective-permute-start(bf16[1792,2048]{1,0:T(8,128)(2,1)} %subtract_convert_fusion.1), channel_id=1, source_target_pairs={{0,28},{4,0},{8,4},{12,8},{16,12},{20,16},{24,20},{28,24},{1,29},{... | collective-permute-start | bytes 22020104 | tf_op jit(solution)/shard_map/ppermute | solution.py:12
  174.1 472.2 %collective-permute-start.2 = (bf16[1792,2048]{1,0:T(8,128)(2,1)}, bf16[1792,2048]{1,0:T(8,128)(2,1)}, u32[]{:S(2)}, u32[]{:S(2)}) collective-permute-start(bf16[1792,2048]{1,0:T(8,128)(2,1)} %subtract_convert_fusion.1), channel_id=1, source_target_pairs={{0,8},{4,12},{8,16},{12,20},{16,24},{20,28},{24,0},{28,4},{1,9},{5... | collective-permute-start | bytes 22020104 | tf_op jit(solution)/shard_map/ppermute | solution.py:12
  175.6 471.5 %collective-permute-start = (bf16[1792,2048]{1,0:T(8,128)(2,1)}, bf16[1792,2048]{1,0:T(8,128)(2,1)}, u32[]{:S(2)}, u32[]{:S(2)}) collective-permute-start(bf16[1792,2048]{1,0:T(8,128)(2,1)} %subtract_convert_fusion.1), channel_id=1, source_target_pairs={{0,4},{4,8},{8,12},{12,16},{16,20},{20,24},{24,28},{28,0},{1,5},{5... | collective-permute-start | bytes 22020104 | tf_op jit(solution)/shard_map/ppermute | solution.py:12
Sparse Core Ops, SparseCore 0:
  8.9 37.1 all-gather.2
  72.6 44.5 reduce-scatter.1
  119.9 34.4 all-gather.4
  674.7 238.1 all-reduce.1
where the time goes:
time: 932 us
  waiting for transfers between devices  826 us (89%)
  other arithmetic  42.8 us (5%)
  matrix products  38.2 us (4%)
  between operations  13.2 us (1%)
    ppermute x4, waiting for transfers between devices, passed_along(): lax.ppermute(x, axis, [(i, (i + by) % devices) for i in range(devices)])  469 us
    psum x1, waiting for transfers between devices, body(): lax.psum(mixed.astype(jnp.float32).astype(jnp.bfloat16), 'blk')  238 us
    reduce_scatter x1, waiting for transfers between devices, body(): lax.psum_scatter((jnp.dot(rows, weight, preferred_element_type=jnp.float3...  44.7 us
    all_gather x1, waiting for transfers between devices, body(): lax.all_gather(tokens, 'shard', axis=0, tiled=True)  38.8 us
    all_gather x1, waiting for transfers between devices, body(): lax.all_gather(resid, 'shard', axis=0, tiled=True)  34.5 us
    convert_element_type x1, other arithmetic, combine(): return (total / 4.0).astype(jnp.bfloat16)  27.4 us
  transfers between devices with their start and end apart: 8, of which 8 were waited for; matrix products, arithmetic and copies ran while one was open for 0% of the time, Pallas kernels for 0%

commit v1 on v0

--- a/solution.py
+++ b/solution.py
@@ -1,3 +1,4 @@
+import functools
 import jax
 import jax.numpy as jnp
 from jax import lax
@@ -5,6 +6,13 @@
 
 FF = 7168
 learn_rate = 2.0
+
+
+def compute_notes_now(block_in, dev_axis):
+    return jnp.sum(lax.all_gather(block_in, axis_name=dev_axis), axis=0)
+
+
+track_groups_in = functools.partial(compute_notes_now, dev_axis="blk")
 
 
 def passed_along(x, axis, by):
@@ -67,7 +75,7 @@
     first_self = combine(stepped, near_left, near_right, numer_of(mix_numer, 0, worker))
     first_right = combine(near_right, stepped, far_right, numer_of(mix_numer, 0, right_worker))
     mixed = combine(first_self, first_left, first_right, numer_of(mix_numer, 1, worker))
-    total = lax.psum(mixed.astype(jnp.float32).astype(jnp.bfloat16), "blk").astype(jnp.float32)
+    total = track_groups_in(mixed.astype(jnp.float32).astype(jnp.bfloat16)).astype(jnp.float32)
     average = total / jnp.float32(workers)
     return (mixed.astype(jnp.float32) - average).astype(jnp.bfloat16)[None]
 

time: 932 us -> 1830 us (1.96)
  waiting for transfers between devices: 826 us -> 1690 us
  other arithmetic: 42.8 us -> 65.8 us
    all_gather x0 -> x1, waiting for transfers between devices: none -> 1110 us  [compute_notes_now(): return jnp.sum(lax.all_gather(block_in, axis_name=dev_axis), axis=0)]
    psum x1 -> x0, waiting for transfers between devices: 238 us -> none  [body(): lax.psum(mixed.astype(jnp.float32).astype(jnp.bfloat16), 'blk')]
    reduce_sum x0 -> x1, other arithmetic: none -> 23 us  [compute_notes_now(): return jnp.sum(lax.all_gather(block_in, axis_name=dev_axis), axis=0)]
where the time goes in v1:
time: 1830 us
  waiting for transfers between devices  1690 us (92%)
  other arithmetic  65.8 us (4%)
  matrix products  38.2 us (2%)
    all_gather x1, waiting for transfers between devices, compute_notes_now(): return jnp.sum(lax.all_gather(block_in, axis_name=dev_axis), axis=0)  1110 us
    ppermute x4, waiting for transfers between devices, passed_along(): lax.ppermute(x, axis, [(i, (i + by) % devices) for i in range(devices)])  467 us
    reduce_scatter x1, waiting for transfers between devices, body(): lax.psum_scatter((jnp.dot(rows, weight, preferred_element_type=jnp.float3...  44.7 us
    all_gather x1, waiting for transfers between devices, body(): lax.all_gather(tokens, 'shard', axis=0, tiled=True)  38.8 us
  transfers between devices with their start and end apart: 8, of which 8 were waited for; matrix products, arithmetic and copies ran while one was open for 0% of the time, Pallas kernels for 0%

profile of v1, /device:TPU:0, one launch (start us, length us, event | category | flops | bytes accessed | tf_op | source)
XLA Modules:
  0.0 1825.6 jit_solution(17866897673565174988)
XLA Ops:
  6.5 0.0 all-gather.5.cloned.1.call-start
  6.5 0.7 all-gather.5.cloned.1.call-update
  7.3 0.0 reduce-scatter.2.cloned.1.call-start
  7.3 38.8 %all-gather.5.cloned.1.call-done = bf16[1024,2048]{1,0:T(8,128)(2,1)} async-done(((bf16[256,2048]{1,0:T(8,128)(2,1)}), bf16[1024,2048]{1,0:T(8,128)(2,1)}) %all-gather.5.cloned.1.call-update) | async-done | bytes 4194320 | tf_op jit(solution)/shard_map/all_gather | solution.py:43
  46.1 11.7 fusion.22
  57.8 0.0 copy-start.2
  57.8 3.0 copy-done.2
  60.8 0.0 copy-start
  60.8 11.6 multiply_convert_fusion.1
  72.4 0.0 reduce-scatter.2.cloned.1.call-update
  72.5 0.0 all-gather.7.cloned.1.call-start
  72.5 44.7 %reduce-scatter.2.cloned.1.call-done = bf16[256,2048]{1,0:T(8,128)(2,1)} async-done(((bf16[1024,2048]{1,0:T(8,128)(2,1)}), bf16[256,2048]{1,0:T(8,128)(2,1)}) %reduce-scatter.2.cloned.1.call-update) | async-done | bytes 1048592 | tf_op jit(solution)/shard_map/reduce_scatter | solution.py:49
  117.2 0.0 copy-done
  117.2 2.6 subtract_convert_fusion.2
  119.8 0.0 all-gather.7.cloned.1.call-update
  119.8 0.0 copy-start.1
  119.8 0.0 all-gather.9.cloned.1.call-start
  119.9 34.5 %all-gather.7.cloned.1.call-done = bf16[1024,2048]{1,0:T(8,128)(2,1)} async-done(((bf16[256,2048]{1,0:T(8,128)(2,1)}), bf16[1024,2048]{1,0:T(8,128)(2,1)}) %all-gather.7.cloned.1.call-update) | async-done | bytes 4194320 | tf_op jit(solution)/shard_map/all_gather | solution.py:61
  154.4 14.9 subtract_convert_fusion.1
  169.3 3.3 collective-permute-start.3
  172.7 0.0 collective-permute-start.2
  172.7 4.7 collective-permute-start.1
  177.4 0.0 collective-permute-start
  177.4 0.0 copy-done.1
  177.4 0.1 dynamic-slice_convert_fusion.2
  177.5 0.6 fusion.19
  178.1 0.6 fusion.21
  178.7 0.6 fusion.20
  179.3 0.6 fusion.18
  179.9 151.5 %collective-permute-done.3 = bf16[1792,2048]{1,0:T(8,128)(2,1)} collective-permute-done((bf16[1792,2048]{1,0:T(8,128)(2,1)}, bf16[1792,2048]{1,0:T(8,128)(2,1)}, u32[]{:S(2)}, u32[]{:S(2)}) %collective-permute-start.3) | collective-permute-done | bytes 7340064 | tf_op jit(solution)/shard_map/ppermute | solution.py:20
  331.4 158.3 %collective-permute-done.2 = bf16[1792,2048]{1,0:T(8,128)(2,1)} collective-permute-done((bf16[1792,2048]{1,0:T(8,128)(2,1)}, bf16[1792,2048]{1,0:T(8,128)(2,1)}, u32[]{:S(2)}, u32[]{:S(2)}) %collective-permute-start.2) | collective-permute-done | bytes 7340064 | tf_op jit(solution)/shard_map/ppermute | solution.py:20
  489.7 155.6 %collective-permute-done.1 = bf16[1792,2048]{1,0:T(8,128)(2,1)} collective-permute-done((bf16[1792,2048]{1,0:T(8,128)(2,1)}, bf16[1792,2048]{1,0:T(8,128)(2,1)}, u32[]{:S(2)}, u32[]{:S(2)}) %collective-permute-start.1) | collective-permute-done | bytes 7340064 | tf_op jit(solution)/shard_map/ppermute | solution.py:20
  645.3 1.8 collective-permute-done
  647.1 27.4 %multiply_convert_fusion = bf16[1792,2048]{1,0:T(8,128)(2,1)} fusion(bf16[1792,2048]{1,0:T(8,128)(2,1)} %collective-permute-done.3, bf16[1792,2048]{1,0:T(8,128)(2,1)} %subtract_convert_fusion.1, bf16[1792,2048]{1,0:T(8,128)(2,1)} %collective-permute-done.1, bf16[1792,2048]{1,0:T(8,128)(2,1)} %collective-permute-done.2, ...), kind=kLoop, calls=%fused_computation.20 | loop fusion | flops 132120576 | bytes 44040240 | tf_op jit(solution)/shard_map/convert_element_type | solution.py:29
  674.5 0.0 all-gather.9.cloned.1.call-update
  674.5 1108.8 %all-gather.9.cloned.1.call-done = bf16[14336,2048]{1,0:T(8,128)(2,1)} async-done(((bf16[1792,2048]{1,0:T(8,128)(2,1)}), bf16[14336,2048]{1,0:T(8,128)(2,1)}) %all-gather.9.cloned.1.call-update) | async-done | bytes 58720272 | tf_op jit(solution)/shard_map/all_gather | solution.py:12
  1783.3 23.0 %reduce_sum.12 = bf16[1792,2048]{1,0:T(8,128)(2,1)} reduce(bf16[8,1792,2048]{2,1,0:T(8,128)(2,1)} %bitcast.24, bf16[]{:T(256)} %constant.60.clone.1), dimensions={0}, to_apply=%region_1.2 | reduce | flops 25690112 | bytes 66060288 | tf_op jit(solution)/shard_map/reduce_sum | solution.py:12
  1806.4 12.7 fusion.12
  (1 shorter events, 0.0 us)
Async XLA Ops:
  6.5 39.6 %all-gather.5.cloned.1.call-start = ((), (), s32[]{:S(2)}) async-start(), calls=%async_computation.1 | async-start | bytes 5242880 | tf_op jit(solution)/shard_map/all_gather | solution.py:43
  7.3 109.9 %reduce-scatter.2.cloned.1.call-start = ((), (), s32[]{:S(2)}) async-start(), calls=%async_computation.2 | async-start | bytes 5242880 | tf_op jit(solution)/shard_map/reduce_scatter | solution.py:49
  57.8 3.1 copy-start.2
  60.8 56.4 %copy-start = (bf16[256,2048]{1,0:T(8,128)(2,1)S(1)}, bf16[256,2048]{1,0:T(8,128)(2,1)}, u32[]{:S(2)}) copy-start(bf16[256,2048]{1,0:T(8,128)(2,1)} %param.6) | copy-start | bytes 3145732
  72.5 82.0 %all-gather.7.cloned.1.call-start = ((), (), s32[]{:S(2)}) async-start(), calls=%async_computation.3 | async-start | bytes 5242880 | tf_op jit(solution)/shard_map/all_gather | solution.py:61
  119.8 57.6 %copy-start.1 = (s32[2,8,3]{1,0,2:T(2,128)S(1)}, s32[2,8,3]{1,0,2:T(2,128)}, u32[]{:S(2)}) copy-start(s32[2,8,3]{1,0,2:T(2,128)} %param.9) | copy-start | bytes 580
  119.8 1663.5 %all-gather.9.cloned.1.call-start = ((), (), s32[]{:S(2)}) async-start(), calls=%async_computation.4 | async-start | bytes 66060288 | tf_op jit(solution)/shard_map/all_gather | solution.py:12
  169.3 162.1 %collective-permute-start.3 = (bf16[1792,2048]{1,0:T(8,128)(2,1)}, bf16[1792,2048]{1,0:T(8,128)(2,1)}, u32[]{:S(2)}, u32[]{:S(2)}) collective-permute-start(bf16[1792,2048]{1,0:T(8,128)(2,1)} %subtract_convert_fusion.1), channel_id=1, source_target_pairs={{0,24},{4,28},{8,0},{12,4},{16,8},{20,12},{24,16},{28,20},{1,25},{... | collective-permute-start | bytes 22020104 | tf_op jit(solution)/shard_map/ppermute | solution.py:20
  172.7 317.0 %collective-permute-start.2 = (bf16[1792,2048]{1,0:T(8,128)(2,1)}, bf16[1792,2048]{1,0:T(8,128)(2,1)}, u32[]{:S(2)}, u32[]{:S(2)}) collective-permute-start(bf16[1792,2048]{1,0:T(8,128)(2,1)} %subtract_convert_fusion.1), channel_id=1, source_target_pairs={{0,8},{4,12},{8,16},{12,20},{16,24},{20,28},{24,0},{28,4},{1,9},{5... | collective-permute-start | bytes 22020104 | tf_op jit(solution)/shard_map/ppermute | solution.py:20
  172.7 472.6 %collective-permute-start.1 = (bf16[1792,2048]{1,0:T(8,128)(2,1)}, bf16[1792,2048]{1,0:T(8,128)(2,1)}, u32[]{:S(2)}, u32[]{:S(2)}) collective-permute-start(bf16[1792,2048]{1,0:T(8,128)(2,1)} %subtract_convert_fusion.1), channel_id=1, source_target_pairs={{0,28},{4,0},{8,4},{12,8},{16,12},{20,16},{24,20},{28,24},{1,29},{... | collective-permute-start | bytes 22020104 | tf_op jit(solution)/shard_map/ppermute | solution.py:20
  177.4 469.7 %collective-permute-start = (bf16[1792,2048]{1,0:T(8,128)(2,1)}, bf16[1792,2048]{1,0:T(8,128)(2,1)}, u32[]{:S(2)}, u32[]{:S(2)}) collective-permute-start(bf16[1792,2048]{1,0:T(8,128)(2,1)} %subtract_convert_fusion.1), channel_id=1, source_target_pairs={{0,4},{4,8},{8,12},{12,16},{16,20},{20,24},{24,28},{28,0},{1,5},{5... | collective-permute-start | bytes 22020104 | tf_op jit(solution)/shard_map/ppermute | solution.py:20
Sparse Core Ops, SparseCore 0:
  8.9 37.1 all-gather.4
  72.6 44.5 reduce-scatter.1
  119.9 34.4 all-gather.6
  674.7 1108.6 all-gather.8
